TPU v7x, 32 devices: a whole 2x2x4 slice. The times are simulated.
32 devices in a mesh: site: 8 (over z, x), dom: 4 (over y, core).
Axes of the slice: x: 2, y: 2, z: 4, core: 2. Of those that a mesh axis runs over, the one named last changes fastest.
Arguments:
- top_partial: float32 [16, 61, 4, 8192], P(None, None, 'dom', 'site'), may hold values from 0.001 to 1
- bottom_partial: float32 [16, 61, 4, 8192], P(None, None, 'dom', 'site'), may hold values from 0.001 to 1
- left_vectors: float32 [256, 61, 61], P('dom'), may hold values from 0.05 to 1
- right_vectors: float32 [256, 61, 61], P('dom'), may hold values from 0.05 to 1
- decay_rates: float32 [256, 61], P('dom'), may hold values from 0.05 to 8
- state_weights: float32 [256, 61], P('dom'), may hold values from 0.002 to 0.05
- part_rates: float32 [256], P('dom'), may hold values from 0.3 to 3
- branch_lengths: float32 [1997], replicated, may hold values from 0.02 to 0.5
- pattern_weights: int32 [4, 8192], P('dom', 'site'), may hold values from 0 to 9
- block_partition: int32 [4, 64], P('dom', 'site'), may hold values from 0 to 255
- chosen_branches: int32 [16], replicated, may hold values from 0 to 1996, as said below
Outputs:
- site_loglik: float32 [16, 4, 8192], P(None, 'dom', 'site')
- part_derivs: float32 [2, 16, 256], P(None, None, 'dom')
- new_lengths: float32 [1997], replicated
Inputs may be any that keep to these rules, and one draw needn't show every extreme that they name: `chosen_branches`: distinct branch numbers.
All inputs are finite; a program needn't handle non-finite values.
Results may differ from a plain program's by a relative error of at most 0.0003.
Values sent between devices are 32-bit elements; how exact they have to be, the bound alone decides.
A program may use at most 64 MiB of HBM per device.

v0:
```python
import functools

import jax
import jax.numpy as jnp
from jax import lax
from jax.experimental import pallas as pl
from jax.experimental.pallas import tpu as pltpu
from jax.sharding import PartitionSpec as P

BLK = 128
MESH = pl.DeviceIdType.MESH
F32 = jnp.float32
BF16 = jnp.bfloat16


def round_up(value, unit):
    return (value + unit - 1) // unit * unit


def split(value):
    high = value.astype(BF16)
    return high, (value - high.astype(F32)).astype(BF16)


def body(
    cfg,
    top_hbm, bottom_hbm, left_hbm, right_hbm,
    decay_hbm, weight_hbm, rate_hbm, lengths_hbm, chosen_hbm,
    pattern_hbm, blocks_hbm,
    like_ref, final_ref,
    top_v, bottom_v, left_v, right_v, req_v, req_s, mine, passed, got,
    top_x, bottom_x, like_v, acc, dom_in, site_out, site_in,
    decay_ref, weight_ref, rate_s, lengths_s, chosen_s, pattern_ref, blocks_s, blocks_ref,
    load_sem, small_sem, req_send, req_recv, req_local, tab_send, tab_recv,
    dom_send, dom_recv, site_send, site_recv,
):
    doms, sites, inner, branches, states, nblk, owned, pad, chunk = cfg
    me = lax.axis_index("dom")
    spot = lax.axis_index("site")
    dom_bits = doms.bit_length() - 1
    outer = sites // inner
    near, far = lax.rem(spot, inner), spot // inner
    nchunk = nblk // chunk
    used = branches * states * nblk

    plane = [(d, x) for d in range(doms) for x in range(inner) if d or x]

    def in_plane(d, x):
        return {"dom": me ^ d, "site": far * inner + lax.rem(near + x, inner)}

    def in_line(k):
        return {"site": lax.rem(far + k, outer) * inner + near}

    loads = [
        pltpu.make_async_copy(left_hbm, left_v, load_sem.at[0]),
        pltpu.make_async_copy(right_hbm, right_v, load_sem.at[1]),
        pltpu.make_async_copy(top_hbm, top_v.at[pl.ds(0, used)], load_sem.at[2]),
        pltpu.make_async_copy(bottom_hbm, bottom_v.at[pl.ds(0, used)], load_sem.at[3]),
    ]
    small = [
        pltpu.make_async_copy(source, dest, small_sem.at[i])
        for i, (source, dest) in enumerate((
            (blocks_hbm, blocks_ref),
            (decay_hbm, decay_ref),
            (weight_hbm, weight_ref),
            (rate_hbm, rate_s),
            (blocks_hbm, blocks_s),
            (lengths_hbm, lengths_s),
            (chosen_hbm, chosen_s),
            (pattern_hbm, pattern_ref),
        ))
    ]

    barrier = pltpu.get_barrier_semaphore()
    for d, x in plane:
        pl.semaphore_signal(barrier, inc=1, device_id=in_plane(d, x), device_id_type=MESH)
    for k in range(1, outer):
        pl.semaphore_signal(barrier, inc=1, device_id=in_line(k), device_id_type=MESH)

    for load in small + loads[:2]:
        load.start()
    req_v[0] = jnp.zeros((1, BLK), jnp.int32)
    tail = top_v.shape[0] - used
    top_v[pl.ds(used, tail), :] = jnp.zeros((tail, BLK), F32)
    bottom_v[pl.ds(used, tail), :] = jnp.zeros((tail, BLK), F32)
    mine[...] = jnp.zeros(mine.shape, F32)

    small[0].wait()
    req_v[0, 0:1, 0:nblk] = blocks_ref[...]
    pl.semaphore_wait(barrier, len(plane) + outer - 1)

    asks = []
    for delta in range(1, doms):
        ask = pltpu.make_async_remote_copy(
            src_ref=req_v.at[0],
            dst_ref=req_v.at[delta],
            send_sem=req_send.at[delta],
            recv_sem=req_recv.at[delta],
            device_id={"dom": me ^ delta},
            device_id_type=MESH,
        )
        ask.start()
        asks.append(ask)
    for load in small[1:] + loads[:2]:
        load.wait()
    loads[2].start()
    loads[3].start()
    for ask in asks:
        ask.wait()
    local = pltpu.make_async_copy(req_v, req_s, req_local)
    local.start()
    local.wait()

    def gather(delta, c=None):
        def step(n, carry):
            relative = req_s[delta, 0, n] - me * owned
            inside = jnp.logical_and(relative >= 0, relative < owned)
            keep = jnp.where(inside, 1.0, 0.0).astype(F32)
            p = jnp.clip(relative, 0, owned - 1)
            mine[delta, n, 0:states, 0:states] = left_v[pl.ds(p, states, stride=owned), :] * keep
            mine[delta, n, 0:states, pad:pad + states] = right_v[pl.ds(p, states, stride=owned), :] * keep
            rate = rate_s[p] * keep
            mine[delta, n, states:states + 1, pad:pad + states] = -decay_ref[pl.ds(p, 1), :] * rate
            mine[delta, n, states + 1:states + 2, pad:pad + states] = (
                weight_ref[pl.ds(p, 1), :] * keep
            )
            return carry

        if c is None:
            lax.fori_loop(0, nblk, step, 0)
        else:
            lax.fori_loop(c * chunk, (c + 1) * chunk, step, 0, unroll=True)

    def convert(n, carry):
        for source, dest in ((top_v, top_x), (bottom_v, bottom_x)):
            for b in range(branches):
                rows = source[pl.ds(b * states * nblk + n, pad, stride=nblk), :]
                high, low = split(rows)
                at = n * (branches // 2) + b // 2
                lanes = (b % 2) * BLK
                dest[at, 0:pad, lanes:lanes + BLK] = high
                dest[at, pad:2 * pad, lanes:lanes + BLK] = low
        return carry

    sends = {}
    for bit in range(dom_bits):
        moves = [d for d in range(doms) if d % (1 << bit) == 0 and (d >> bit) & 1]
        for d in sorted(moves, reverse=True):
            to = d ^ (1 << bit)
            for c in range(nchunk):
                at = pl.ds(c * chunk, chunk)
                sends[(bit, d, c)] = pltpu.make_async_remote_copy(
                    src_ref=(mine if bit == 0 else passed).at[d, at],
                    dst_ref=got.at[bit, to, at],
                    send_sem=tab_send.at[bit, d, c],
                    recv_sem=tab_recv.at[bit, to, c],
                    device_id={"dom": me ^ (1 << bit)},
                    device_id_type=MESH,
                )

    def forward(bit, d):
        for c in range(nchunk):
            at = pl.ds(c * chunk, chunk)
            total = mine[d, at]
            for earlier in range(bit):
                sends[(earlier, d | (1 << earlier), c)].wait_recv()
                total = total + got[earlier, d, at]
            passed[d, at] = total
            sends[(bit, d, c)].start()

    for d in reversed(range(doms)):
        if d & 1 and d > 1:
            for c in range(nchunk):
                gather(d, c)
                sends[(0, d, c)].start()
    for d in reversed(range(2, doms)):
        if not d & 1:
            gather(d)
    for bit in range(1, dom_bits):
        for d in reversed(range(doms)):
            if d % (1 << bit) == 0 and (d >> bit) & 1:
                forward(bit, d)
    for c in range(nchunk):
        gather(1, c)
        sends[(0, 1, c)].start()
    gather(0)
    loads[2].wait()
    loads[3].wait()
    lax.fori_loop(0, nblk, convert, 0)

    acc[...] = jnp.zeros(acc.shape, F32)
    lane = lax.broadcasted_iota(jnp.int32, (2 * branches, BLK), 1)
    times = [lengths_s[chosen_s[b]] for b in range(branches)]

    def block(n, carry):
        tile = mine[0, n]
        for bit in range(dom_bits):
            tile = tile + got[bit, 0, n]
        turned = jnp.transpose(tile)
        w_row = tile[states + 1:states + 2, pad:2 * pad]
        l_high, l_low = split(turned[0:pad, :] * w_row)
        r_high, r_low = split(tile[:, pad:2 * pad])
        l_all = jnp.concatenate([l_high, l_high, l_low], axis=1)
        r_all = jnp.concatenate([r_high, r_high, r_low], axis=1)
        expo = jnp.broadcast_to(turned[pad:2 * pad, states:states + 1], (pad, BLK))
        for half in range(branches // 2):
            at = n * (branches // 2) + half
            t_x = top_x[at]
            b_x = bottom_x[at]
            lefts = jnp.dot(
                l_all, jnp.concatenate([t_x, t_x[0:pad]], axis=0), preferred_element_type=F32
            )
            rights = jnp.dot(
                r_all, jnp.concatenate([b_x, b_x[0:pad]], axis=0), preferred_element_type=F32
            )
            joint = lefts * rights
            for side in range(2):
                b = 2 * half + side
                decayed = joint[:, side * BLK:(side + 1) * BLK] * jnp.exp(expo * times[b])
                once = decayed * expo
                twice = once * expo
                like_v[0, b:b + 1, :] = jnp.sum(decayed, axis=0, keepdims=True)
                like_v[1, b:b + 1, :] = jnp.sum(once, axis=0, keepdims=True)
                like_v[2, b:b + 1, :] = jnp.sum(twice, axis=0, keepdims=True)
        like0 = like_v[0]
        first_d = like_v[1] / like0
        second_d = like_v[2] / like0 - first_d * first_d
        w_sites = pattern_ref[pl.ds(n, 1), :].astype(F32)
        like_ref[pl.ds(n, branches, stride=nblk), :] = like0
        both = jnp.concatenate([first_d, second_d], axis=0) * w_sites
        sums = jnp.sum(both, axis=1, keepdims=True)
        p = blocks_s[0, n]
        for d in range(doms):
            hit = jnp.logical_and(lane + d * owned == p, lane < owned)
            hit = jnp.logical_or(hit, lane == owned)
            acc[d] = acc[d] + jnp.where(hit, sums, 0.0)
        return carry

    for c in range(nchunk):
        for bit in range(dom_bits):
            sends[(bit, 1 << bit, c)].wait_recv()
        lax.fori_loop(c * chunk, (c + 1) * chunk, block, 0, unroll=True)

    scatter = []
    for d, x in reversed(plane):
        copy = pltpu.make_async_remote_copy(
            src_ref=acc.at[me ^ d],
            dst_ref=dom_in.at[me * inner + near],
            send_sem=dom_send.at[d * inner + x],
            recv_sem=dom_recv.at[d * inner + x],
            device_id=in_plane(d, x),
            device_id_type=MESH,
        )
        copy.start()
        scatter.append(copy)
    dom_in[me * inner + near] = acc[me]
    for copy in scatter:
        copy.wait_recv()
    total = dom_in[0]
    for d in range(1, doms * inner):
        total = total + dom_in[d]
    site_out[...] = total
    spread = []
    for k in range(1, outer):
        copy = pltpu.make_async_remote_copy(
            src_ref=site_out,
            dst_ref=site_in.at[far],
            send_sem=site_send.at[k],
            recv_sem=site_recv.at[k],
            device_id=in_line(k),
            device_id_type=MESH,
        )
        copy.start()
        spread.append(copy)
    site_in[far] = total
    for copy in spread:
        copy.wait_recv()
    total = site_in[0]
    for z in range(1, outer):
        total = total + site_in[z]

    sums = total[:, owned:owned + 1]
    ratio = sums[0:branches] / sums[branches:2 * branches]
    row = lax.broadcasted_iota(jnp.int32, (branches, BLK), 0)
    old = jnp.zeros((branches, BLK), F32)
    for b in range(branches):
        old = jnp.where(row == b, times[b], old)
    final_ref[0:2 * branches, :] = total
    final_ref[2 * branches:3 * branches, :] = old - ratio

    for copy in scatter + spread:
        copy.wait_send()
    for copy in sends.values():
        copy.wait_send()


def write(
    cfg, like_ref, final_ref, pattern_ref, chosen_s, lengths_ref, loglik_ref, share_ref, new_ref
):
    branches, nblk, owned = cfg
    weights = pattern_ref[...].astype(F32)
    for b in range(branches):
        rows = pl.ds(b * nblk, nblk)
        loglik_ref[rows, :] = weights * jnp.log(like_ref[rows, :])
    share_ref[...] = final_ref[0:2 * branches, 0:owned]
    new = lengths_ref[...]
    place = lax.broadcasted_iota(jnp.int32, new.shape, 1)
    for b in range(branches):
        value = final_ref[2 * branches + b:2 * branches + b + 1, 0:1]
        new = jnp.where(place == chosen_s[b], value, new)
    new_ref[...] = new


def on_device(
    top_partial,
    bottom_partial,
    left_vectors,
    right_vectors,
    decay_rates,
    state_weights,
    part_rates,
    branch_lengths,
    pattern_weights,
    block_partition,
    chosen_branches,
):
    doms = lax.axis_size("dom")
    sites = lax.axis_size("site")
    branches, states, _, sites_here = top_partial.shape
    nblk = sites_here // BLK
    owned = left_vectors.shape[0]
    tree = branch_lengths.shape[0]
    pad = round_up(states + 2, 64)
    chunk = 2 if nblk % 2 == 0 else 1
    nchunk = nblk // chunk
    dom_bits = doms.bit_length() - 1
    inner = 2 if sites % 2 == 0 else 1
    outer = sites // inner
    used = branches * states * nblk
    room = used + (pad - states) * nblk
    cfg = (doms, sites, inner, branches, states, nblk, owned, pad, chunk)
    hbm = pl.BlockSpec(memory_space=pl.ANY)
    vmem = pl.BlockSpec(memory_space=pltpu.VMEM)
    smem = pl.BlockSpec(memory_space=pltpu.SMEM)
    tile = (pad, 2 * pad)
    dma = pltpu.SemaphoreType.DMA
    pattern = pattern_weights.reshape(nblk, BLK)
    like, final = pl.pallas_call(
        functools.partial(body, cfg),
        out_shape=(
            jax.ShapeDtypeStruct((branches * nblk, BLK), F32),
            jax.ShapeDtypeStruct((3 * branches, BLK), F32),
        ),
        in_specs=[hbm] * 11,
        out_specs=(vmem, vmem),
        scratch_shapes=[
            pltpu.VMEM((room, BLK), F32),
            pltpu.VMEM((room, BLK), F32),
            pltpu.VMEM((states * owned, states), F32),
            pltpu.VMEM((states * owned, states), F32),
            pltpu.VMEM((doms, 1, BLK), jnp.int32),
            pltpu.SMEM((doms, 1, BLK), jnp.int32),
            pltpu.VMEM((doms, nblk) + tile, F32),
            pltpu.VMEM((doms, nblk) + tile, F32),
            pltpu.VMEM((dom_bits, doms, nblk) + tile, F32),
            pltpu.VMEM((nblk * branches // 2, 2 * pad, 2 * BLK), BF16),
            pltpu.VMEM((nblk * branches // 2, 2 * pad, 2 * BLK), BF16),
            pltpu.VMEM((3, branches, BLK), F32),
            pltpu.VMEM((doms, 2 * branches, BLK), F32),
            pltpu.VMEM((doms * inner, 2 * branches, BLK), F32),
            pltpu.VMEM((2 * branches, BLK), F32),
            pltpu.VMEM((outer, 2 * branches, BLK), F32),
            pltpu.VMEM((owned, states), F32),
            pltpu.VMEM((owned, states), F32),
            pltpu.SMEM((owned,), F32),
            pltpu.SMEM((tree,), F32),
            pltpu.SMEM((branches,), jnp.int32),
            pltpu.VMEM((nblk, BLK), jnp.int32),
            pltpu.SMEM((1, nblk), jnp.int32),
            pltpu.VMEM((1, nblk), jnp.int32),
            dma((4,)),
            dma((8,)),
            dma((doms,)),
            dma((doms,)),
            dma,
            dma((dom_bits, doms, nchunk)),
            dma((dom_bits, doms, nchunk)),
            dma((doms * inner,)),
            dma((doms * inner,)),
            dma((outer,)),
            dma((outer,)),
        ],
        compiler_params=pltpu.CompilerParams(
            collective_id=0, has_side_effects=True, vmem_limit_bytes=56 * 1024 * 1024
        ),
    )(
        top_partial.reshape(used, BLK),
        bottom_partial.reshape(used, BLK),
        jnp.swapaxes(left_vectors, 0, 1).reshape(states * owned, states),
        jnp.swapaxes(right_vectors, 0, 1).reshape(states * owned, states),
        decay_rates,
        state_weights,
        part_rates,
        branch_lengths,
        chosen_branches,
        pattern,
        block_partition,
    )
    loglik, share, new = pl.pallas_call(
        functools.partial(write, (branches, nblk, owned)),
        out_shape=(
            jax.ShapeDtypeStruct((branches * nblk, BLK), F32),
            jax.ShapeDtypeStruct((2 * branches, owned), F32),
            jax.ShapeDtypeStruct((1, tree), F32),
        ),
        in_specs=[vmem, vmem, vmem, smem, vmem],
        out_specs=(vmem, vmem, vmem),
    )(like, final, pattern, chosen_branches, branch_lengths.reshape(1, tree))
    return (
        loglik.reshape(branches, 1, sites_here),
        share.reshape(2, branches, owned),
        new.reshape(tree),
    )


def solution(mesh):
    return jax.shard_map(
        on_device,
        mesh=mesh,
        in_specs=(
            P(None, None, "dom", "site"),
            P(None, None, "dom", "site"),
            P("dom", None, None),
            P("dom", None, None),
            P("dom", None),
            P("dom", None),
            P("dom"),
            P(),
            P("dom", "site"),
            P("dom", "site"),
            P(),
        ),
        out_specs=(P(None, "dom", "site"), P(None, None, "dom"), P()),
        check_vma=False,
    )
```

profile of v0, /device:TPU:0, one launch (start us, length us, event | category | flops | bytes accessed | tf_op | source)
XLA Modules:
  0.0 29.5 jit_solution(3768964509149300711)
XLA Ops:
  0.6 27.1 %shard_map.130 = (f32[128,128]{1,0:T(8,128)}, f32[48,128]{1,0:T(8,128)}) custom-call(f32[7808,128]{1,0:T(8,128)} %bitcast.13, f32[7808,128]{1,0:T(8,128)} %bitcast.14, f32[3904,61]{1,0:T(8,128)} %bitcast.15, f32[3904,61]{1,0:T(8,128)} %bitcast.16, f32[64,61]{1,0:T(8,128)} %decay_hbm.1, f32[64,61]{1,0:T(8,128)} %weight_hbm.1, f32[64]{0:T(128)} %rate_hbm.1, ...), custom_call_target="tpu_custom_call" | custom-call | tf_op jit(solution)/shard_map/pallas_call | solution.py:348
  27.8 1.7 %shard_map.131 = (f32[128,128]{1,0:T(8,128)}, f32[32,64]{1,0:T(8,128)}, f32[1,1997]{1,0:T(1,128)}) custom-call(f32[128,128]{1,0:T(8,128)} %get-tuple-element.8.like_ref, f32[48,128]{1,0:T(8,128)} %get-tuple-element.9.final_ref, s32[8,128]{1,0:T(8,128)} %bitcast.19, s32[16]{0:T(128)} %chosen_s.1, f32[1,1997]{1,0:T(1,128)} %bitcast.17), custom_call_target="tpu_custom_call" | custom-call | tf_op jit(solution)/shard_map/pallas_call | solution.py:409
where the time goes:
time: 29.6 us; the launch traced here: 29.5 us
  Pallas kernels  28.8 us (97%)
  between operations  0.64 us (2%)
    pallas_call x1, Pallas kernels, on_device(): pl.pallas_call(functools.partial(body, cfg), out_shape=(jax.ShapeDtypeStr...  27.1 us
    pallas_call x1, Pallas kernels, on_device(): pl.pallas_call(functools.partial(write, (branches, nblk, owned)), out_sha...  1.7 us

commit v1 on v0

v1 whole, which is shorter than its diff:
```python
import functools

import jax
import jax.numpy as jnp
from jax import lax
from jax.experimental import pallas as pl
from jax.experimental.pallas import tpu as pltpu
from jax.sharding import PartitionSpec as P

BLK = 128
MESH = pl.DeviceIdType.MESH
F32 = jnp.float32
LOG2E = 1.4426950408889634
BF16 = jnp.bfloat16


def round_up(value, unit):
    return (value + unit - 1) // unit * unit


def split(value):
    high = value.astype(BF16)
    return high, (value - high.astype(F32)).astype(BF16)


def thirds(value):
    high = value.astype(BF16)
    rest = value - high.astype(F32)
    middle = rest.astype(BF16)
    return high, middle, (rest - middle.astype(F32)).astype(BF16)


def settle(ref, sem):
    pltpu.make_async_copy(ref, ref, sem).wait()


def body(
    cfg,
    top_hbm, bottom_hbm, left_hbm, right_hbm,
    decay_hbm, weight_hbm, rate_hbm, lengths_hbm, chosen_hbm,
    pattern_hbm, blocks_hbm, row_hbm,
    loglik_ref, share_ref, new_ref,
    top_v, bottom_v, tables_v, req_v, req_s, mine, passed, got,
    top_x, bottom_x, like_v, parts_v, pay_v, pay_in, ids_v, hot_v, old_v, pick_v, row_v,
    modes_v, rate_s, lengths_s, chosen_s, pattern_ref, blocks_s, blocks_ref,
    load_sem, small_sem, gossip, req_send, req_recv, tab_send, near_recv, pass_recv, far_recv,
    ids_send, ids_recv, pay_send, pay_recv,
):
    doms, sites, inner, branches, states, nblk, owned, pad, group = cfg
    me = lax.axis_index("dom")
    spot = lax.axis_index("site")
    dom_bits = doms.bit_length() - 1
    outer = sites // inner
    near, far = lax.rem(spot, inner), spot // inner
    kinds = 2 * branches
    rows = nblk // group

    def at_site(x, z):
        return lax.rem(far + z, outer) * inner + lax.rem(near + x, inner)

    def greet(sem):
        @pl.when(far > 0)
        def _():
            pl.semaphore_signal(
                sem, inc=1, device_id={"site": spot - inner}, device_id_type=MESH
            )

        @pl.when(far < outer - 1)
        def _():
            pl.semaphore_signal(
                sem, inc=1, device_id={"site": spot + inner}, device_id_type=MESH
            )

        for x in range(1, inner):
            pl.semaphore_signal(
                sem, inc=1, device_id={"site": at_site(x, 0)}, device_id_type=MESH
            )
        for d in reversed(range(1, doms)):
            pl.semaphore_signal(sem, inc=1, device_id={"dom": me ^ d}, device_id_type=MESH)

    around = (
        doms - 1 + inner - 1 + jnp.where(far > 0, 1, 0) + jnp.where(far < outer - 1, 1, 0)
    )

    tables = [
        pltpu.make_async_copy(source, tables_v.at[i, :, pl.ds(0, owned), :], load_sem.at[0])
        for i, source in enumerate((left_hbm, right_hbm))
    ]
    tops = [
        pltpu.make_async_copy(
            top_hbm.at[:, :, n, :], top_v.at[n, :, pl.ds(0, states), :], load_sem.at[1]
        )
        for n in range(nblk)
    ]
    bottoms = [
        pltpu.make_async_copy(
            bottom_hbm.at[:, :, n, :], bottom_v.at[n, :, pl.ds(0, states), :], load_sem.at[2]
        )
        for n in range(nblk)
    ]
    modes = [
        pltpu.make_async_copy(source, modes_v.at[i], load_sem.at[3])
        for i, source in enumerate((decay_hbm, weight_hbm))
    ]
    small = [
        pltpu.make_async_copy(source, dest, small_sem.at[i])
        for i, (source, dest) in enumerate((
            (blocks_hbm, blocks_ref),
            (rate_hbm, rate_s),
            (blocks_hbm, blocks_s),
            (lengths_hbm, lengths_s),
            (chosen_hbm, chosen_s),
            (pattern_hbm, pattern_ref),
            (row_hbm, row_v),
        ))
    ]

    small[0].start()
    barrier = pltpu.get_barrier_semaphore()
    greet(barrier)
    for load in modes + tables + small[1:] + tops:
        load.start()
    req_v[0] = jnp.zeros((1, BLK), jnp.int32)
    for side in (top_v, bottom_v):
        for n in range(nblk):
            side[n, :, states:pad, :] = jnp.zeros((branches, pad - states, BLK), F32)
    mine[...] = jnp.zeros(mine.shape, F32)

    small[0].wait()
    req_v[0, 0:1, 0:nblk] = blocks_ref[...]
    pl.semaphore_wait(barrier, around)

    for kind, dest in enumerate((req_s, req_v)):
        for delta in reversed(range(1, doms)):
            pltpu.make_async_remote_copy(
                src_ref=req_v.at[0],
                dst_ref=dest.at[delta],
                send_sem=req_send.at[kind],
                recv_sem=req_recv.at[kind],
                device_id={"dom": me ^ delta},
                device_id_type=MESH,
            ).start()
    greet(gossip.at[0])

    def convert(source, dest):
        def step(n, carry):
            for b in range(branches):
                high, low = split(source[n, b])
                at = n * (branches // 2) + b // 2
                lanes = (b % 2) * BLK
                dest[at, 0:pad, lanes:lanes + BLK] = high
                dest[at, pad:2 * pad, lanes:lanes + BLK] = low
            return carry

        lax.fori_loop(0, nblk, step, 0)

    settle(top_v.at[:, :, pl.ds(0, states), :], load_sem.at[1])
    for load in bottoms:
        load.start()
    convert(top_v, top_x)
    settle(modes_v, load_sem.at[3])
    settle(tables_v.at[:, :, pl.ds(0, owned), :], load_sem.at[0])
    for load in small[1:]:
        load.wait()
    settle(req_s.at[pl.ds(1, doms - 1)], req_recv.at[0])

    def gather(delta, n):
        wanted = blocks_s[0, n] if delta == 0 else req_s[delta, 0, n]
        relative = wanted - me * owned
        inside = jnp.logical_and(relative >= 0, relative < owned)
        keep = jnp.where(inside, 1.0, 0.0).astype(F32)
        p = jnp.clip(relative, 0, owned - 1)
        mine[delta, n, 0:states, 0:states] = tables_v[0, :, p, :] * keep
        mine[delta, n, 0:states, pad:pad + states] = tables_v[1, :, p, :] * keep
        rate = rate_s[p] * keep
        mine[delta, n, states:states + 1, pad:pad + states] = -modes_v[0, pl.ds(p, 1), :] * rate
        mine[delta, n, states + 1:states + 2, pad:pad + states] = (
            modes_v[1, pl.ds(p, 1), :] * keep
        )

    def send(bit, d, n):
        to = d ^ (1 << bit)
        if bit == 0:
            arrived = near_recv.at[0] if to == 0 else pass_recv.at[to, n]
        else:
            arrived = far_recv.at[bit, n] if to == 0 else pass_recv.at[to, n]
        return pltpu.make_async_remote_copy(
            src_ref=(mine if bit == 0 else passed).at[d, n],
            dst_ref=got.at[bit, to, n],
            send_sem=tab_send.at[d],
            recv_sem=arrived,
            device_id={"dom": me ^ (1 << bit)},
            device_id_type=MESH,
        )

    def forward(bit, d, n):
        total = mine[d, n]
        for earlier in range(bit):
            send(earlier, d | (1 << earlier), n).wait_recv()
            total = total + got[earlier, d, n]
        passed[d, n] = total
        send(bit, d, n).start()

    for d in reversed(range(2, doms)):
        if d & 1:
            for n in range(nblk):
                gather(d, n)
                send(0, d, n).start()
    for d in reversed(range(2, doms)):
        if not d & 1:
            for n in range(nblk):
                gather(d, n)
    for bit in range(1, dom_bits):
        for d in reversed(range(doms)):
            if d % (1 << bit) == 0 and (d >> bit) & 1:
                for n in range(nblk):
                    forward(bit, d, n)
    pl.semaphore_wait(gossip.at[0], around)
    greet(gossip.at[1])
    for n in range(nblk):
        gather(1, n)
    for n in range(nblk):
        send(0, 1, n).start()
    for n in range(nblk):
        gather(0, n)
    pl.semaphore_wait(gossip.at[1], around)
    greet(gossip.at[2])
    settle(bottom_v.at[:, :, pl.ds(0, states), :], load_sem.at[2])
    convert(bottom_v, bottom_x)
    for step in range(3, outer):
        pl.semaphore_wait(gossip.at[step - 1], around)
        greet(gossip.at[step])
    settle(req_v.at[pl.ds(1, doms - 1)], req_recv.at[1])
    settle(got.at[0, 0], near_recv.at[0])
    times = [lengths_s[chosen_s[b]] for b in range(branches)]
    ones = jnp.ones((16, 3 * BLK), BF16)

    def block(n):
        tile = mine[0, n]
        for bit in range(dom_bits):
            tile = tile + got[bit, 0, n]
        turned = jnp.transpose(tile)
        w_row = tile[states + 1:states + 2, pad:2 * pad]
        l_high, l_low = split(turned[0:pad, :] * w_row)
        r_high, r_low = split(tile[:, pad:2 * pad])
        none = jnp.zeros((pad, pad), BF16)
        l_all = jnp.concatenate([
            jnp.concatenate([l_high, l_high], axis=1), jnp.concatenate([l_low, none], axis=1)
        ], axis=0)
        r_all = jnp.concatenate([
            jnp.concatenate([r_high, r_high], axis=1), jnp.concatenate([r_low, none], axis=1)
        ], axis=0)
        expo = jnp.broadcast_to(turned[pad:2 * pad, states:states + 1], (pad, BLK))
        power = expo * LOG2E
        for half in range(branches // 2):
            at = n * (branches // 2) + half
            lefts = jnp.dot(l_all, top_x[at], preferred_element_type=F32)
            rights = jnp.dot(r_all, bottom_x[at], preferred_element_type=F32)
            joint = (lefts[0:pad] + lefts[pad:2 * pad]) * (rights[0:pad] + rights[pad:2 * pad])
            for side in range(2):
                b = 2 * half + side
                decayed = joint[:, side * BLK:(side + 1) * BLK] * jnp.exp2(power * times[b])
                once = decayed * expo
                twice = once * expo
                like_v[0, b:b + 1, :] = jnp.sum(decayed, axis=0, keepdims=True)
                like_v[1, b:b + 1, :] = jnp.sum(once, axis=0, keepdims=True)
                like_v[2, b:b + 1, :] = jnp.sum(twice, axis=0, keepdims=True)
        like0 = like_v[0]
        first_d = like_v[1] / like0
        second_d = like_v[2] / like0 - first_d * first_d
        w_sites = pattern_ref[pl.ds(n, 1), :].astype(F32)
        loglik_ref[pl.ds(n, branches, stride=nblk), :] = like0
        both = jnp.concatenate([first_d, second_d], axis=0) * w_sites
        q = n % group
        for i, part in enumerate(thirds(both)):
            parts_v[n // group, q * kinds:(q + 1) * kinds, i * BLK:(i + 1) * BLK] = part
        if q == group - 1:
            sums = lax.dot_general(
                ones, parts_v[n // group], (((1,), (1,)), ((), ())), preferred_element_type=F32
            )
            pay_v[n // group:n // group + 1, :] = sums[0:1]

    for n in range(nblk):
        for bit in range(1, dom_bits):
            send(bit, 1 << bit, n).wait_recv()
        if n == min(2, nblk - 1):
            pl.semaphore_wait(gossip.at[outer - 1], around)
            for z in reversed(range(outer)):
                for x in range(inner):
                    if x or z:
                        pltpu.make_async_remote_copy(
                            src_ref=req_v,
                            dst_ref=ids_v.at[spot],
                            send_sem=ids_send.at[0],
                            recv_sem=ids_recv.at[0],
                            device_id={"site": at_site(x, z)},
                            device_id_type=MESH,
                        ).start()
            ids_v[spot] = req_v[...]
        block(n)

    peers = [(d, x, z) for d in range(doms) for x in range(inner) for z in range(outer)][1:]
    peers.sort(key=lambda peer: -(min(peer[2], outer - peer[2]) + peer[1] + peer[0] // 2))
    for d, x, z in peers:
        pltpu.make_async_remote_copy(
            src_ref=pay_v.at[pl.ds(0, rows)],
            dst_ref=pay_in.at[spot * doms + d, pl.ds(0, rows)],
            send_sem=pay_send.at[0],
            recv_sem=pay_recv.at[0],
            device_id={"dom": me ^ d, "site": at_site(x, z)},
            device_id_type=MESH,
        ).start()
    pay_in[spot * doms, 0:rows] = pay_v[0:rows]

    weights = pattern_ref[...].astype(F32)
    for b in range(branches):
        lines = pl.ds(b * nblk, nblk)
        loglik_ref[lines, :] = weights * jnp.log(loglik_ref[lines, :])
    settle(ids_v.at[pl.ds(1, sites - 1)], ids_recv.at[0])
    ids = ids_v[...].reshape(sites * doms, BLK)
    lane = lax.broadcasted_iota(jnp.int32, (sites * doms, BLK), 1)
    for n in range(nblk):
        hit = jnp.logical_and(ids[:, n:n + 1] - me * owned == lane, lane < owned)
        hit = jnp.logical_or(hit, lane == owned)
        start = (n // group) * sites * doms
        hot_v[n % group, start:start + sites * doms, :] = jnp.where(hit, 1.0, 0.0).astype(BF16)
    row = lax.broadcasted_iota(jnp.int32, (branches, BLK), 0)
    old = jnp.zeros((branches, BLK), F32)
    for b in range(branches):
        old = jnp.where(row == b, times[b], old)
    old_v[...] = old
    tree = new_ref.shape[1]
    place = lax.broadcasted_iota(jnp.int32, (1, tree), 1)
    kept = row_v[...]
    for b in range(branches):
        here = place == chosen_s[b]
        pick_v[b:b + 1, :] = jnp.where(here, 1.0, 0.0)
        kept = jnp.where(here, 0.0, kept)
    row_v[...] = kept

    settle(pay_in.at[pl.ds(1, sites * doms - 1), pl.ds(0, rows)], pay_recv.at[0])
    lines = jnp.concatenate([pay_in[:, h, :] for h in range(rows)], axis=0)
    flipped = jnp.transpose(lines)
    stacked = jnp.zeros((3 * kinds, BLK), F32)
    for q in range(group):
        third = thirds(flipped[q * kinds:(q + 1) * kinds, :])
        stacked = stacked + jnp.dot(
            jnp.concatenate(third, axis=0), hot_v[q], preferred_element_type=F32
        )
    total = stacked[0:kinds] + stacked[kinds:2 * kinds] + stacked[2 * kinds:3 * kinds]
    share_ref[...] = total[:, 0:owned]
    sums = total[:, owned:owned + 1]
    value = (old_v[...] - sums[0:branches] / sums[branches:kinds])[:, 0:1]
    chosen = jnp.where(pick_v[...] > 0.0, value, 0.0)
    new_ref[...] = row_v[...] + jnp.sum(chosen, axis=0, keepdims=True)

    for kind in range(2):
        settle(req_v.at[pl.ds(1, doms - 1)], req_send.at[kind])
    settle(ids_v.at[pl.ds(1, sites - 1)], ids_send.at[0])
    settle(pay_in.at[pl.ds(1, sites * doms - 1), pl.ds(0, rows)], pay_send.at[0])
    for d in range(1, doms):
        settle(mine.at[d], tab_send.at[d])


def store(loglik_v, share_v, new_v, loglik_ref, share_ref, new_ref, sem):
    copies = [
        pltpu.make_async_copy(source, dest, sem.at[i])
        for i, (source, dest) in enumerate((
            (new_v, new_ref), (share_v, share_ref), (loglik_v, loglik_ref)
        ))
    ]
    for copy in copies:
        copy.start()
    for copy in copies:
        copy.wait()


def on_device(
    top_partial,
    bottom_partial,
    left_vectors,
    right_vectors,
    decay_rates,
    state_weights,
    part_rates,
    branch_lengths,
    pattern_weights,
    block_partition,
    chosen_branches,
):
    doms = lax.axis_size("dom")
    sites = lax.axis_size("site")
    branches, states, _, sites_here = top_partial.shape
    nblk = sites_here // BLK
    owned = left_vectors.shape[0]
    tree = branch_lengths.shape[0]
    pad = round_up(states + 2, 64)
    dom_bits = doms.bit_length() - 1
    inner = 2 if sites % 2 == 0 else 1
    outer = sites // inner
    held = round_up(owned, 8) + 8
    kinds = 2 * branches
    group = BLK // kinds
    rows = nblk // group
    cfg = (doms, sites, inner, branches, states, nblk, owned, pad, group)
    hbm = pl.BlockSpec(memory_space=pltpu.HBM)
    vmem = pl.BlockSpec(memory_space=pltpu.VMEM)
    tile = (pad, 2 * pad)
    dma = pltpu.SemaphoreType.DMA
    pattern = pattern_weights.reshape(nblk, BLK)
    loglik, share, new = pl.pallas_call(
        functools.partial(body, cfg),
        out_shape=(
            pltpu.VMEM((branches * nblk, BLK), F32),
            pltpu.VMEM((kinds, owned), F32),
            pltpu.VMEM((1, tree), F32),
        ),
        in_specs=[hbm] * 12,
        out_specs=(vmem, vmem, vmem),
        scratch_shapes=[
            pltpu.VMEM((nblk, branches, pad, BLK), F32),
            pltpu.VMEM((nblk, branches, pad, BLK), F32),
            pltpu.VMEM((2, states, held, states), F32),
            pltpu.VMEM((doms, 1, BLK), jnp.int32),
            pltpu.SMEM((doms, 1, BLK), jnp.int32),
            pltpu.VMEM((doms, nblk) + tile, F32),
            pltpu.VMEM((doms, nblk) + tile, F32),
            pltpu.VMEM((dom_bits, doms, nblk) + tile, F32),
            pltpu.VMEM((nblk * branches // 2, 2 * pad, 2 * BLK), BF16),
            pltpu.VMEM((nblk * branches // 2, 2 * pad, 2 * BLK), BF16),
            pltpu.VMEM((3, branches, BLK), F32),
            pltpu.VMEM((rows, group * kinds, 3 * BLK), BF16),
            pltpu.VMEM((round_up(rows, 8), BLK), F32),
            pltpu.VMEM((sites * doms, round_up(rows, 8), BLK), F32),
            pltpu.VMEM((sites, doms, 1, BLK), jnp.int32),
            pltpu.VMEM((group, rows * sites * doms, BLK), BF16),
            pltpu.VMEM((branches, BLK), F32),
            pltpu.VMEM((branches, tree), F32),
            pltpu.VMEM((1, tree), F32),
            pltpu.VMEM((2, owned, states), F32),
            pltpu.SMEM((owned,), F32),
            pltpu.SMEM((tree,), F32),
            pltpu.SMEM((branches,), jnp.int32),
            pltpu.VMEM((nblk, BLK), jnp.int32),
            pltpu.SMEM((1, nblk), jnp.int32),
            pltpu.VMEM((1, nblk), jnp.int32),
            dma((4,)),
            dma((7,)),
            pltpu.SemaphoreType.REGULAR((outer,)),
            dma((2,)),
            dma((2,)),
            dma((doms,)),
            dma((1,)),
            dma((doms, nblk)),
            dma((dom_bits, nblk)),
            dma((1,)),
            dma((1,)),
            dma((1,)),
            dma((1,)),
        ],
        compiler_params=pltpu.CompilerParams(
            collective_id=0, has_side_effects=True, vmem_limit_bytes=56 * 1024 * 1024
        ),
    )(
        top_partial.reshape(branches, states, nblk, BLK),
        bottom_partial.reshape(branches, states, nblk, BLK),
        jnp.swapaxes(left_vectors, 0, 1),
        jnp.swapaxes(right_vectors, 0, 1),
        decay_rates,
        state_weights,
        part_rates,
        branch_lengths,
        chosen_branches,
        pattern,
        block_partition,
        branch_lengths.reshape(1, tree),
    )
    loglik, share, new = pl.pallas_call(
        store,
        out_shape=(
            jax.ShapeDtypeStruct((branches * nblk, BLK), F32),
            jax.ShapeDtypeStruct((kinds, owned), F32),
            jax.ShapeDtypeStruct((1, tree), F32),
        ),
        in_specs=[vmem] * 3,
        out_specs=[hbm] * 3,
        scratch_shapes=[dma((3,))],
        compiler_params=pltpu.CompilerParams(vmem_limit_bytes=1024 * 1024),
    )(loglik, share, new)
    return (
        loglik.reshape(branches, 1, sites_here),
        share.reshape(2, branches, owned),
        new.reshape(tree),
    )


def solution(mesh):
    return jax.shard_map(
        on_device,
        mesh=mesh,
        in_specs=(
            P(None, None, "dom", "site"),
            P(None, None, "dom", "site"),
            P("dom", None, None),
            P("dom", None, None),
            P("dom", None),
            P("dom", None),
            P("dom"),
            P(),
            P("dom", "site"),
            P("dom", "site"),
            P(),
        ),
        out_specs=(P(None, "dom", "site"), P(None, None, "dom"), P()),
        check_vma=False,
    )
```

time: 29.6 us -> 24.8 us (0.84)
  Pallas kernels: 28.8 us -> 24.1 us
    pallas_call x2, Pallas kernels: 28.8 us -> 24.1 us  [the longest x1 23.4 us: on_device(): pl.pallas_call(functools.partial(body, cfg), out_shape=(pltpu.VMEM((branc...]
where the time goes in v1:
time: 24.8 us; the launch traced here: 24.7 us
  Pallas kernels  24.1 us (97%)
  between operations  0.64 us (3%)
    pallas_call x1, Pallas kernels, on_device(): pl.pallas_call(functools.partial(body, cfg), out_shape=(pltpu.VMEM((branc...  23.4 us
    pallas_call x1, Pallas kernels, on_device(): pl.pallas_call(store, out_shape=(jax.ShapeDtypeStruct((branches * nblk, B...  0.67 us

profile of v1, /device:TPU:0, one launch (start us, length us, event | category | flops | bytes accessed | tf_op | source)
XLA Modules:
  0.0 24.7 jit_solution(5843266491974172304)
XLA Ops:
  0.6 23.4 %shard_map.130 = (f32[128,128]{1,0:T(8,128)S(1)}, f32[32,64]{1,0:T(8,128)S(1)}, f32[1,1997]{1,0:T(1,128)S(1)}) custom-call(f32[16,61,8,128]{3,2,1,0:T(8,128)} %bitcast.9, f32[16,61,8,128]{3,2,1,0:T(8,128)} %bitcast.10, f32[61,64,61]{2,1,0:T(8,128)} %bitcast.11, f32[61,64,61]{2,1,0:T(8,128)} %bitcast.12, f32[64,61]{1,0:T(8,128)} %decay_hbm.1, ...), custom_call_target="tpu_custom_call" | custom-call | tf_op jit(solution)/shard_map/pallas_call | solution.py:411
  24.0 0.7 %shard_map.131 = (f32[128,128]{1,0:T(8,128)}, f32[32,64]{1,0:T(8,128)}, f32[1,1997]{1,0:T(1,128)}) custom-call(f32[128,128]{1,0:T(8,128)S(1)} %get-tuple-element.9.loglik_v, f32[32,64]{1,0:T(8,128)S(1)} %get-tuple-element.10.share_v, f32[1,1997]{1,0:T(1,128)S(1)} %get-tuple-element.11.new_v), custom_call_target="tpu_custom_call" | custom-call | tf_op jit(solution)/shard_map/pallas_call | solution.py:478

commit v2 on v1

--- a/solution.py
+++ b/solution.py
@@ -40,10 +40,10 @@
     decay_hbm, weight_hbm, rate_hbm, lengths_hbm, chosen_hbm,
     pattern_hbm, blocks_hbm, row_hbm,
     loglik_ref, share_ref, new_ref,
-    top_v, bottom_v, tables_v, req_v, req_s, mine, passed, got,
+    top_v, bottom_v, tables_v, req_v, req_s, mine, passed, got, lone,
     top_x, bottom_x, like_v, parts_v, pay_v, pay_in, ids_v, hot_v, old_v, pick_v, row_v,
     modes_v, rate_s, lengths_s, chosen_s, pattern_ref, blocks_s, blocks_ref,
-    load_sem, small_sem, gossip, req_send, req_recv, tab_send, near_recv, pass_recv, far_recv,
+    load_sem, small_sem, gossip, req_send, req_recv, tab_send, lone_send, near_recv, pass_recv, far_recv,
     ids_send, ids_recv, pay_send, pay_recv,
 ):
     doms, sites, inner, branches, states, nblk, owned, pad, group = cfg
@@ -54,6 +54,9 @@
     near, far = lax.rem(spot, inner), spot // inner
     kinds = 2 * branches
     rows = nblk // group
+    slot = round_up(rows, 8)
+    sent = states + 1
+    early = nblk // 2
 
     def at_site(x, z):
         return lax.rem(far + z, outer) * inner + lax.rem(near + x, inner)
@@ -78,17 +81,20 @@
         for d in reversed(range(1, doms)):
             pl.semaphore_signal(sem, inc=1, device_id={"dom": me ^ d}, device_id_type=MESH)
 
+    odd = lax.rem(me, 2) == 1
     around = (
         doms - 1 + inner - 1 + jnp.where(far > 0, 1, 0) + jnp.where(far < outer - 1, 1, 0)
     )
 
     tables = [
-        pltpu.make_async_copy(source, tables_v.at[i, :, pl.ds(0, owned), :], load_sem.at[0])
+        pltpu.make_async_copy(source, tables_v.at[pl.ds(i * states, states), pl.ds(0, owned), :], load_sem.at[0])
         for i, source in enumerate((left_hbm, right_hbm))
     ]
     tops = [
         pltpu.make_async_copy(
-            top_hbm.at[:, :, n, :], top_v.at[n, :, pl.ds(0, states), :], load_sem.at[1]
+            top_hbm.at[:, :, n, :],
+            top_v.at[n, :, pl.ds(0, states), :],
+            load_sem.at[1 if n < early else 4],
         )
         for n in range(nblk)
     ]
@@ -118,16 +124,26 @@
     small[0].start()
     barrier = pltpu.get_barrier_semaphore()
     greet(barrier)
-    for load in modes + tables + small[1:] + tops:
+    for load in modes + tables + small[1:]:
         load.start()
     req_v[0] = jnp.zeros((1, BLK), jnp.int32)
     for side in (top_v, bottom_v):
         for n in range(nblk):
             side[n, :, states:pad, :] = jnp.zeros((branches, pad - states, BLK), F32)
-    mine[...] = jnp.zeros(mine.shape, F32)
+    for bit in range(dom_bits):
+        for d in range(0, doms, 2 << bit):
+            for n in range(nblk):
+                got[bit, d, n, sent:pad, :] = jnp.zeros((pad - sent, 2 * pad), F32)
+    lone[...] = jnp.zeros(lone.shape, F32)
+    for bit in range(1, dom_bits):
+        got[bit, 0, 0] = jnp.zeros((pad, 2 * pad), F32)
+    for d in range(0, doms):
+        mine[d, :, sent:pad, :] = jnp.zeros((nblk, pad - sent, 2 * pad), F32)
 
     small[0].wait()
     req_v[0, 0:1, 0:nblk] = blocks_ref[...]
+    for load in tops:
+        load.start()
     pl.semaphore_wait(barrier, around)
 
     for kind, dest in enumerate((req_s, req_v)):
@@ -141,8 +157,10 @@
                 device_id_type=MESH,
             ).start()
     greet(gossip.at[0])
-
-    def convert(source, dest):
+    for load in bottoms:
+        load.start()
+
+    def convert(source, dest, first, last):
         def step(n, carry):
             for b in range(branches):
                 high, low = split(source[n, b])
@@ -152,138 +170,199 @@
                 dest[at, pad:2 * pad, lanes:lanes + BLK] = low
             return carry
 
-        lax.fori_loop(0, nblk, step, 0)
-
-    settle(top_v.at[:, :, pl.ds(0, states), :], load_sem.at[1])
-    for load in bottoms:
-        load.start()
-    convert(top_v, top_x)
+        lax.fori_loop(first, last, step, 0)
+
+    settle(top_v.at[pl.ds(0, early), :, pl.ds(0, states), :], load_sem.at[1])
+    convert(top_v, top_x, 0, early)
     settle(modes_v, load_sem.at[3])
-    settle(tables_v.at[:, :, pl.ds(0, owned), :], load_sem.at[0])
+    settle(tables_v.at[:, pl.ds(0, owned), :], load_sem.at[0])
     for load in small[1:]:
         load.wait()
     settle(req_s.at[pl.ds(1, doms - 1)], req_recv.at[0])
 
-    def gather(delta, n):
+    held = tables_v.shape[1]
+    flat = tables_v.reshape(2 * states * held, states)
+
+    def pick(delta, n):
         wanted = blocks_s[0, n] if delta == 0 else req_s[delta, 0, n]
         relative = wanted - me * owned
         inside = jnp.logical_and(relative >= 0, relative < owned)
         keep = jnp.where(inside, 1.0, 0.0).astype(F32)
         p = jnp.clip(relative, 0, owned - 1)
-        mine[delta, n, 0:states, 0:states] = tables_v[0, :, p, :] * keep
-        mine[delta, n, 0:states, pad:pad + states] = tables_v[1, :, p, :] * keep
-        rate = rate_s[p] * keep
-        mine[delta, n, states:states + 1, pad:pad + states] = -modes_v[0, pl.ds(p, 1), :] * rate
-        mine[delta, n, states + 1:states + 2, pad:pad + states] = (
-            modes_v[1, pl.ds(p, 1), :] * keep
+        left = jnp.concatenate(
+            [flat[pl.ds(p, states, stride=held), :], modes_v[1, pl.ds(p, 1), :]], axis=0
         )
+        right = jnp.concatenate(
+            [flat[pl.ds(states * held + p, states, stride=held), :], modes_v[0, pl.ds(p, 1), :] * -rate_s[p]], axis=0
+        )
+        gap = jnp.zeros((sent, pad - states), F32)
+        return jnp.concatenate([left * keep, gap, right * keep, gap], axis=1)
+
+    def gather(delta, wanted, after=None):
+        ready = pick(delta, wanted[0])
+        for i, n in enumerate(wanted):
+            coming = pick(delta, wanted[i + 1]) if i + 1 < len(wanted) else None
+            mine[delta, n, 0:sent, :] = ready
+            if after is not None:
+                after(delta, n)
+            ready = coming
 
     def send(bit, d, n):
         to = d ^ (1 << bit)
         if bit == 0:
-            arrived = near_recv.at[0] if to == 0 else pass_recv.at[to, n]
+            arrived = near_recv.at[0] if to == 0 else pass_recv.at[to // 2 - 1, n]
         else:
-            arrived = far_recv.at[bit, n] if to == 0 else pass_recv.at[to, n]
+            arrived = far_recv.at[bit - 1, n] if to == 0 else pass_recv.at[to // 2 - 1, n]
         return pltpu.make_async_remote_copy(
-            src_ref=(mine if bit == 0 else passed).at[d, n],
-            dst_ref=got.at[bit, to, n],
-            send_sem=tab_send.at[d],
+            src_ref=(mine if bit == 0 else passed).at[d, n, pl.ds(0, sent)],
+            dst_ref=got.at[bit, to, n, pl.ds(0, sent)],
+            send_sem=tab_send.at[d - 1] if n or d == 1 else lone_send.at[1],
             recv_sem=arrived,
             device_id={"dom": me ^ (1 << bit)},
             device_id_type=MESH,
         )
 
+    def straight(d, n):
+        pltpu.make_async_remote_copy(
+            src_ref=mine.at[d, n, pl.ds(0, sent)],
+            dst_ref=lone.at[d, pl.ds(0, sent)],
+            send_sem=lone_send.at[0],
+            recv_sem=near_recv.at[1],
+            device_id={"dom": me ^ d},
+            device_id_type=MESH,
+        ).start()
+
     def forward(bit, d, n):
-        total = mine[d, n]
+        total = mine[d, n, 0:sent, :]
         for earlier in range(bit):
             send(earlier, d | (1 << earlier), n).wait_recv()
-            total = total + got[earlier, d, n]
-        passed[d, n] = total
+            total = total + got[earlier, d, n, 0:sent, :]
+        passed[d, n, 0:sent, :] = total
         send(bit, d, n).start()
+
+    rest = list(range(1, nblk))
+    for d in reversed(range(2, doms)):
+        gather(d, [0])
+
+    @pl.when(odd)
+    def _():
+        for d in range(2, doms):
+            if d & 1:
+                send(0, d, 0).start()
+            else:
+                straight(d, 0)
+
+    @pl.when(jnp.logical_not(odd))
+    def _():
+        for d in range(2, doms):
+            if d & 1:
+                straight(d, 0)
 
     for d in reversed(range(2, doms)):
         if d & 1:
-            for n in range(nblk):
-                gather(d, n)
-                send(0, d, n).start()
+            gather(d, rest, lambda d, n: send(0, d, n).start())
     for d in reversed(range(2, doms)):
         if not d & 1:
-            for n in range(nblk):
-                gather(d, n)
+            gather(d, rest)
     for bit in range(1, dom_bits):
         for d in reversed(range(doms)):
             if d % (1 << bit) == 0 and (d >> bit) & 1:
-                for n in range(nblk):
+                pl.when(jnp.logical_not(odd))(functools.partial(forward, bit, d, 0))
+                for n in rest:
                     forward(bit, d, n)
     pl.semaphore_wait(gossip.at[0], around)
     greet(gossip.at[1])
-    for n in range(nblk):
-        gather(1, n)
-    for n in range(nblk):
+    gather(1, [0] + rest)
+    for n in [0] + rest:
         send(0, 1, n).start()
-    for n in range(nblk):
-        gather(0, n)
-    pl.semaphore_wait(gossip.at[1], around)
-    greet(gossip.at[2])
+    gather(0, [0] + rest)
+    settle(top_v.at[pl.ds(early, nblk - early), :, pl.ds(0, states), :], load_sem.at[4])
+    convert(top_v, top_x, early, nblk)
     settle(bottom_v.at[:, :, pl.ds(0, states), :], load_sem.at[2])
-    convert(bottom_v, bottom_x)
-    for step in range(3, outer):
-        pl.semaphore_wait(gossip.at[step - 1], around)
-        greet(gossip.at[step])
+    convert(bottom_v, bottom_x, 0, nblk)
     settle(req_v.at[pl.ds(1, doms - 1)], req_recv.at[1])
-    settle(got.at[0, 0], near_recv.at[0])
     times = [lengths_s[chosen_s[b]] for b in range(branches)]
-    ones = jnp.ones((16, 3 * BLK), BF16)
+    for h in range(rows):
+        parts_v[h, 0:2 * kinds, :] = jnp.zeros((2 * kinds, 2 * BLK), BF16)
+    ones = jnp.ones((16, 2 * BLK), BF16)
 
     def block(n):
         tile = mine[0, n]
         for bit in range(dom_bits):
             tile = tile + got[bit, 0, n]
+        if n == 0:
+            for d in range(2, doms):
+                tile = tile + lone[d]
         turned = jnp.transpose(tile)
-        w_row = tile[states + 1:states + 2, pad:2 * pad]
+        w_row = tile[states:states + 1, 0:pad]
         l_high, l_low = split(turned[0:pad, :] * w_row)
         r_high, r_low = split(tile[:, pad:2 * pad])
-        none = jnp.zeros((pad, pad), BF16)
-        l_all = jnp.concatenate([
-            jnp.concatenate([l_high, l_high], axis=1), jnp.concatenate([l_low, none], axis=1)
-        ], axis=0)
-        r_all = jnp.concatenate([
-            jnp.concatenate([r_high, r_high], axis=1), jnp.concatenate([r_low, none], axis=1)
-        ], axis=0)
+        l_all = jnp.concatenate([l_high, l_high, l_low], axis=1)
+        r_all = jnp.concatenate([r_high, r_high, r_low], axis=1)
         expo = jnp.broadcast_to(turned[pad:2 * pad, states:states + 1], (pad, BLK))
         power = expo * LOG2E
         for half in range(branches // 2):
             at = n * (branches // 2) + half
-            lefts = jnp.dot(l_all, top_x[at], preferred_element_type=F32)
-            rights = jnp.dot(r_all, bottom_x[at], preferred_element_type=F32)
-            joint = (lefts[0:pad] + lefts[pad:2 * pad]) * (rights[0:pad] + rights[pad:2 * pad])
+            t_x = top_x[at]
+            b_x = bottom_x[at]
+            lefts = jnp.dot(
+                l_all, jnp.concatenate([t_x, t_x[0:pad]], axis=0), preferred_element_type=F32
+            )
+            rights = jnp.dot(
+                r_all, jnp.concatenate([b_x, b_x[0:pad]], axis=0), preferred_element_type=F32
+            )
+            joint = lefts * rights
             for side in range(2):
                 b = 2 * half + side
                 decayed = joint[:, side * BLK:(side + 1) * BLK] * jnp.exp2(power * times[b])
                 once = decayed * expo
                 twice = once * expo
-                like_v[0, b:b + 1, :] = jnp.sum(decayed, axis=0, keepdims=True)
-                like_v[1, b:b + 1, :] = jnp.sum(once, axis=0, keepdims=True)
-                like_v[2, b:b + 1, :] = jnp.sum(twice, axis=0, keepdims=True)
-        like0 = like_v[0]
-        first_d = like_v[1] / like0
-        second_d = like_v[2] / like0 - first_d * first_d
+                like_v[n % 2, 0, b:b + 1, :] = jnp.sum(decayed, axis=0, keepdims=True)
+                like_v[n % 2, 1, b:b + 1, :] = jnp.sum(once, axis=0, keepdims=True)
+                like_v[n % 2, 2, b:b + 1, :] = jnp.sum(twice, axis=0, keepdims=True)
+        like0 = like_v[n % 2, 0]
+        first_d = like_v[n % 2, 1] / like0
+        second_d = like_v[n % 2, 2] / like0 - first_d * first_d
         w_sites = pattern_ref[pl.ds(n, 1), :].astype(F32)
         loglik_ref[pl.ds(n, branches, stride=nblk), :] = like0
         both = jnp.concatenate([first_d, second_d], axis=0) * w_sites
-        q = n % group
-        for i, part in enumerate(thirds(both)):
+        q = group - 1 - n % group
+        for i, part in enumerate(split(both)):
             parts_v[n // group, q * kinds:(q + 1) * kinds, i * BLK:(i + 1) * BLK] = part
-        if q == group - 1:
-            sums = lax.dot_general(
-                ones, parts_v[n // group], (((1,), (1,)), ((), ())), preferred_element_type=F32
-            )
-            pay_v[n // group:n // group + 1, :] = sums[0:1]
-
-    for n in range(nblk):
+
+    def sums_of(h, count):
+        return lax.dot_general(
+            ones,
+            parts_v[h, 0:count * kinds],
+            (((1,), (1,)), ((), ())),
+            preferred_element_type=F32,
+        )[0:1]
+
+    def arrive(n):
         for bit in range(1, dom_bits):
             send(bit, 1 << bit, n).wait_recv()
-        if n == min(2, nblk - 1):
+
+    @pl.when(odd)
+    def _():
+        settle(lone.at[pl.ds(2, doms - 2), pl.ds(0, sent)], near_recv.at[1])
+
+    pl.when(jnp.logical_not(odd))(functools.partial(arrive, 0))
+    alone = nblk // 2
+    pl.semaphore_wait(gossip.at[1], around)
+    greet(gossip.at[2])
+    for n in range(0, alone, 2):
+        if n:
+            arrive(n)
+        else:
+            settle(got.at[0, 0, :, pl.ds(0, sent)], near_recv.at[0])
+        arrive(n + 1)
+        block(n)
+        block(n + 1)
+        if n == 0:
+            for step in range(3, outer):
+                pl.semaphore_wait(gossip.at[step - 1], around)
+                greet(gossip.at[step])
+        if n == 2:
             pl.semaphore_wait(gossip.at[outer - 1], around)
             for z in reversed(range(outer)):
                 for x in range(inner):
@@ -297,20 +376,28 @@
                             device_id_type=MESH,
                         ).start()
             ids_v[spot] = req_v[...]
+
+    for n in range(alone, nblk):
+        arrive(n)
+        if n == nblk - 2:
+            for h in range(rows):
+                pay_v[h:h + 1, :] = sums_of(h, group)
         block(n)
+    late = min(2, group) * kinds
+    pay_v[rows - 1:rows, 0:late] = sums_of(rows - 1, min(2, group))[:, 0:late]
 
     peers = [(d, x, z) for d in range(doms) for x in range(inner) for z in range(outer)][1:]
     peers.sort(key=lambda peer: -(min(peer[2], outer - peer[2]) + peer[1] + peer[0] // 2))
     for d, x, z in peers:
         pltpu.make_async_remote_copy(
             src_ref=pay_v.at[pl.ds(0, rows)],
-            dst_ref=pay_in.at[spot * doms + d, pl.ds(0, rows)],
+            dst_ref=pay_in.at[pl.ds(pl.multiple_of((spot * doms + d) * slot, slot), rows)],
             send_sem=pay_send.at[0],
             recv_sem=pay_recv.at[0],
             device_id={"dom": me ^ d, "site": at_site(x, z)},
             device_id_type=MESH,
         ).start()
-    pay_in[spot * doms, 0:rows] = pay_v[0:rows]
+    pay_in[pl.ds(pl.multiple_of(spot * doms * slot, slot), rows), :] = pay_v[0:rows]
 
     weights = pattern_ref[...].astype(F32)
     for b in range(branches):
@@ -321,9 +408,11 @@
     lane = lax.broadcasted_iota(jnp.int32, (sites * doms, BLK), 1)
     for n in range(nblk):
         hit = jnp.logical_and(ids[:, n:n + 1] - me * owned == lane, lane < owned)
-        hit = jnp.logical_or(hit, lane == owned)
         start = (n // group) * sites * doms
-        hot_v[n % group, start:start + sites * doms, :] = jnp.where(hit, 1.0, 0.0).astype(BF16)
+        hot_v[group - 1 - n % group, start:start + sites * doms, 0:BLK] = (
+            jnp.where(hit, 1.0, 0.0).astype(BF16)
+        )
+    hot_v[:, :, BLK:2 * BLK] = jnp.ones((group, rows * sites * doms, BLK), BF16)
     row = lax.broadcasted_iota(jnp.int32, (branches, BLK), 0)
     old = jnp.zeros((branches, BLK), F32)
     for b in range(branches):
@@ -338,10 +427,10 @@
         kept = jnp.where(here, 0.0, kept)
     row_v[...] = kept
 
-    settle(pay_in.at[pl.ds(1, sites * doms - 1), pl.ds(0, rows)], pay_recv.at[0])
-    lines = jnp.concatenate([pay_in[:, h, :] for h in range(rows)], axis=0)
+    settle(pay_in.at[pl.ds(0, (sites * doms - 1) * rows)], pay_recv.at[0])
+    lines = jnp.concatenate([pay_in[pl.ds(h, sites * doms, stride=slot), :] for h in range(rows)], axis=0)
     flipped = jnp.transpose(lines)
-    stacked = jnp.zeros((3 * kinds, BLK), F32)
+    stacked = jnp.zeros((3 * kinds, 2 * BLK), F32)
     for q in range(group):
         third = thirds(flipped[q * kinds:(q + 1) * kinds, :])
         stacked = stacked + jnp.dot(
@@ -349,17 +438,23 @@
         )
     total = stacked[0:kinds] + stacked[kinds:2 * kinds] + stacked[2 * kinds:3 * kinds]
     share_ref[...] = total[:, 0:owned]
-    sums = total[:, owned:owned + 1]
-    value = (old_v[...] - sums[0:branches] / sums[branches:kinds])[:, 0:1]
-    chosen = jnp.where(pick_v[...] > 0.0, value, 0.0)
-    new_ref[...] = row_v[...] + jnp.sum(chosen, axis=0, keepdims=True)
+    sums = total[:, BLK:2 * BLK]
+    value = old_v[...] - sums[0:branches] / sums[branches:kinds]
+    for start in range(0, tree, BLK):
+        width = min(BLK, tree - start)
+        lanes = slice(start, start + width)
+        chosen = jnp.where(pick_v[:, lanes] > 0.0, value[:, 0:width], 0.0)
+        new_ref[:, lanes] = row_v[:, lanes] + jnp.sum(chosen, axis=0, keepdims=True)
 
     for kind in range(2):
         settle(req_v.at[pl.ds(1, doms - 1)], req_send.at[kind])
     settle(ids_v.at[pl.ds(1, sites - 1)], ids_send.at[0])
-    settle(pay_in.at[pl.ds(1, sites * doms - 1), pl.ds(0, rows)], pay_send.at[0])
+    settle(pay_in.at[pl.ds(0, (sites * doms - 1) * rows)], pay_send.at[0])
+    for i in range(2):
+        settle(lone.at[pl.ds(2, doms // 2 - 1), pl.ds(0, sent)], lone_send.at[i])
     for d in range(1, doms):
-        settle(mine.at[d], tab_send.at[d])
+        start = 0 if d == 1 else 1
+        settle(mine.at[d, pl.ds(start, nblk - start), pl.ds(0, sent)], tab_send.at[d - 1])
 
 
 def store(loglik_v, share_v, new_v, loglik_ref, share_ref, new_ref, sem):
@@ -420,20 +515,21 @@
         scratch_shapes=[
             pltpu.VMEM((nblk, branches, pad, BLK), F32),
             pltpu.VMEM((nblk, branches, pad, BLK), F32),
-            pltpu.VMEM((2, states, held, states), F32),
+            pltpu.VMEM((2 * states, held, states), F32),
             pltpu.VMEM((doms, 1, BLK), jnp.int32),
             pltpu.SMEM((doms, 1, BLK), jnp.int32),
             pltpu.VMEM((doms, nblk) + tile, F32),
             pltpu.VMEM((doms, nblk) + tile, F32),
             pltpu.VMEM((dom_bits, doms, nblk) + tile, F32),
+            pltpu.VMEM((doms,) + tile, F32),
             pltpu.VMEM((nblk * branches // 2, 2 * pad, 2 * BLK), BF16),
             pltpu.VMEM((nblk * branches // 2, 2 * pad, 2 * BLK), BF16),
-            pltpu.VMEM((3, branches, BLK), F32),
-            pltpu.VMEM((rows, group * kinds, 3 * BLK), BF16),
+            pltpu.VMEM((2, 3, branches, BLK), F32),
+            pltpu.VMEM((rows, group * kinds, 2 * BLK), BF16),
             pltpu.VMEM((round_up(rows, 8), BLK), F32),
-            pltpu.VMEM((sites * doms, round_up(rows, 8), BLK), F32),
+            pltpu.VMEM((sites * doms * round_up(rows, 8), BLK), F32),
             pltpu.VMEM((sites, doms, 1, BLK), jnp.int32),
-            pltpu.VMEM((group, rows * sites * doms, BLK), BF16),
+            pltpu.VMEM((group, rows * sites * doms, 2 * BLK), BF16),
             pltpu.VMEM((branches, BLK), F32),
             pltpu.VMEM((branches, tree), F32),
             pltpu.VMEM((1, tree), F32),
@@ -444,15 +540,16 @@
             pltpu.VMEM((nblk, BLK), jnp.int32),
             pltpu.SMEM((1, nblk), jnp.int32),
             pltpu.VMEM((1, nblk), jnp.int32),
-            dma((4,)),
+            dma((5,)),
             dma((7,)),
             pltpu.SemaphoreType.REGULAR((outer,)),
             dma((2,)),
             dma((2,)),
-            dma((doms,)),
-            dma((1,)),
-            dma((doms, nblk)),
-            dma((dom_bits, nblk)),
+            dma((doms - 1,)),
+            dma((2,)),
+            dma((2,)),
+            dma((doms // 2 - 1, nblk)),
+            dma((dom_bits - 1, nblk)),
             dma((1,)),
             dma((1,)),
             dma((1,)),

time: 24.8 us -> 23.4 us (0.944)
  Pallas kernels: 24.1 us -> 22.6 us
    pallas_call x1, Pallas kernels: 23.4 us -> 21.9 us  [on_device(): pl.pallas_call(functools.partial(body, cfg), out_shape=(pltpu.VMEM((branc...]
where the time goes in v2:
time: 23.4 us; the launch traced here: 23.3 us
  Pallas kernels  22.6 us (97%)
  between operations  0.64 us (3%)
    pallas_call x1, Pallas kernels, on_device(): pl.pallas_call(functools.partial(body, cfg), out_shape=(pltpu.VMEM((branc...  21.9 us
    pallas_call x1, Pallas kernels, on_device(): pl.pallas_call(store, out_shape=(jax.ShapeDtypeStruct((branches * nblk, B...  0.67 us

profile of v2, /device:TPU:0, one launch (start us, length us, event | category | flops | bytes accessed | tf_op | source)
XLA Modules:
  0.0 23.3 jit_solution(12390471021493832309)
XLA Ops:
  0.6 21.9 %shard_map.130 = (f32[128,128]{1,0:T(8,128)S(1)}, f32[32,64]{1,0:T(8,128)S(1)}, f32[1,1997]{1,0:T(1,128)S(1)}) custom-call(f32[16,61,8,128]{3,2,1,0:T(8,128)} %bitcast.9, f32[16,61,8,128]{3,2,1,0:T(8,128)} %bitcast.10, f32[61,64,61]{2,1,0:T(8,128)} %bitcast.11, f32[61,64,61]{2,1,0:T(8,128)} %bitcast.12, f32[64,61]{1,0:T(8,128)} %decay_hbm.1, ...), custom_call_target="tpu_custom_call" | custom-call | tf_op jit(solution)/shard_map/pallas_call | solution.py:506
  22.6 0.7 %shard_map.131 = (f32[128,128]{1,0:T(8,128)}, f32[32,64]{1,0:T(8,128)}, f32[1,1997]{1,0:T(1,128)}) custom-call(f32[128,128]{1,0:T(8,128)S(1)} %get-tuple-element.9.loglik_v, f32[32,64]{1,0:T(8,128)S(1)} %get-tuple-element.10.share_v, f32[1,1997]{1,0:T(1,128)S(1)} %get-tuple-element.11.new_v), custom_call_target="tpu_custom_call" | custom-call | tf_op jit(solution)/shard_map/pallas_call | solution.py:575

commit v3 on v2

--- a/solution.py
+++ b/solution.py
@@ -40,7 +40,7 @@
     decay_hbm, weight_hbm, rate_hbm, lengths_hbm, chosen_hbm,
     pattern_hbm, blocks_hbm, row_hbm,
     loglik_ref, share_ref, new_ref,
-    top_v, bottom_v, tables_v, req_v, req_s, mine, passed, got, lone,
+    top_v, bottom_v, tables_v, req_v, req_s, mine, passed, near_v, far_v, lone,
     top_x, bottom_x, like_v, parts_v, pay_v, pay_in, ids_v, hot_v, old_v, pick_v, row_v,
     modes_v, rate_s, lengths_s, chosen_s, pattern_ref, blocks_s, blocks_ref,
     load_sem, small_sem, gossip, req_send, req_recv, tab_send, lone_send, near_recv, pass_recv, far_recv,
@@ -49,13 +49,12 @@
     doms, sites, inner, branches, states, nblk, owned, pad, group = cfg
     me = lax.axis_index("dom")
     spot = lax.axis_index("site")
-    dom_bits = doms.bit_length() - 1
     outer = sites // inner
     near, far = lax.rem(spot, inner), spot // inner
     kinds = 2 * branches
     rows = nblk // group
     slot = round_up(rows, 8)
-    sent = states + 1
+    sent = states
     early = nblk // 2
 
     def at_site(x, z):
@@ -130,15 +129,13 @@
     for side in (top_v, bottom_v):
         for n in range(nblk):
             side[n, :, states:pad, :] = jnp.zeros((branches, pad - states, BLK), F32)
-    for bit in range(dom_bits):
-        for d in range(0, doms, 2 << bit):
-            for n in range(nblk):
-                got[bit, d, n, sent:pad, :] = jnp.zeros((pad - sent, 2 * pad), F32)
-    lone[...] = jnp.zeros(lone.shape, F32)
-    for bit in range(1, dom_bits):
-        got[bit, 0, 0] = jnp.zeros((pad, 2 * pad), F32)
-    for d in range(0, doms):
-        mine[d, :, sent:pad, :] = jnp.zeros((nblk, pad - sent, 2 * pad), F32)
+    for n in range(nblk):
+        near_v[0, n, sent:pad, :] = jnp.zeros((pad - sent, 2 * pad), F32)
+        for k in range(1, doms // 2):
+            far_v[k, n, sent:pad, :] = jnp.zeros((pad - sent, 2 * pad), F32)
+    for d in range(2, doms):
+        lone[d, sent:pad, :] = jnp.zeros((pad - sent, 2 * pad), F32)
+    mine[0, :, sent:pad, :] = jnp.zeros((nblk, pad - sent, 2 * pad), F32)
 
     small[0].wait()
     req_v[0, 0:1, 0:nblk] = blocks_ref[...]
@@ -189,42 +186,45 @@
         inside = jnp.logical_and(relative >= 0, relative < owned)
         keep = jnp.where(inside, 1.0, 0.0).astype(F32)
         p = jnp.clip(relative, 0, owned - 1)
-        left = jnp.concatenate(
-            [flat[pl.ds(p, states, stride=held), :], modes_v[1, pl.ds(p, 1), :]], axis=0
+        left = jnp.concatenate([
+            flat[pl.ds(p, states, stride=held), :],
+            modes_v[0, pl.ds(p, 1), :] * -rate_s[p],
+            jnp.zeros((pad - states - 1, states), F32),
+        ], axis=0)
+        right = flat[pl.ds(states * held + p, states, stride=held), :]
+        turned = jnp.transpose(
+            jnp.concatenate([left, jnp.zeros((pad, 2 * pad - states), F32)], axis=1)
         )
-        right = jnp.concatenate(
-            [flat[pl.ds(states * held + p, states, stride=held), :], modes_v[0, pl.ds(p, 1), :] * -rate_s[p]], axis=0
-        )
-        gap = jnp.zeros((sent, pad - states), F32)
-        return jnp.concatenate([left * keep, gap, right * keep, gap], axis=1)
-
-    def gather(delta, wanted, after=None):
-        ready = pick(delta, wanted[0])
-        for i, n in enumerate(wanted):
-            coming = pick(delta, wanted[i + 1]) if i + 1 < len(wanted) else None
+        scale = jnp.concatenate([
+            modes_v[1, pl.ds(p, 1), :] * keep,
+            jnp.full((1, 1), keep),
+            jnp.zeros((1, pad - states - 1), F32),
+        ], axis=1)
+        gap = jnp.zeros((states, pad - states), F32)
+        return jnp.concatenate([turned[0:states, :] * scale, right * keep, gap], axis=1)
+
+    def gather(wanted, after=None):
+        ready = pick(*wanted[0])
+        for i, (delta, n) in enumerate(wanted):
+            coming = pick(*wanted[i + 1]) if i + 1 < len(wanted) else None
             mine[delta, n, 0:sent, :] = ready
             if after is not None:
                 after(delta, n)
             ready = coming
 
-    def send(bit, d, n):
-        to = d ^ (1 << bit)
-        if bit == 0:
-            arrived = near_recv.at[0] if to == 0 else pass_recv.at[to // 2 - 1, n]
-        else:
-            arrived = far_recv.at[bit - 1, n] if to == 0 else pass_recv.at[to // 2 - 1, n]
-        return pltpu.make_async_remote_copy(
-            src_ref=(mine if bit == 0 else passed).at[d, n, pl.ds(0, sent)],
-            dst_ref=got.at[bit, to, n, pl.ds(0, sent)],
-            send_sem=tab_send.at[d - 1] if n or d == 1 else lone_send.at[1],
-            recv_sem=arrived,
-            device_id={"dom": me ^ (1 << bit)},
-            device_id_type=MESH,
-        )
-
-    def straight(d, n):
+    def beside(d, n):
         pltpu.make_async_remote_copy(
             src_ref=mine.at[d, n, pl.ds(0, sent)],
+            dst_ref=near_v.at[d ^ 1, n, pl.ds(0, sent)],
+            send_sem=tab_send.at[1 if d == 1 else 0],
+            recv_sem=near_recv.at[0] if d == 1 else pass_recv.at[n - 1],
+            device_id={"dom": me ^ 1},
+            device_id_type=MESH,
+        ).start()
+
+    def straight(d):
+        pltpu.make_async_remote_copy(
+            src_ref=mine.at[d, 0, pl.ds(0, sent)],
             dst_ref=lone.at[d, pl.ds(0, sent)],
             send_sem=lone_send.at[0],
             recv_sem=near_recv.at[1],
@@ -232,50 +232,45 @@
             device_id_type=MESH,
         ).start()
 
-    def forward(bit, d, n):
-        total = mine[d, n, 0:sent, :]
-        for earlier in range(bit):
-            send(earlier, d | (1 << earlier), n).wait_recv()
-            total = total + got[earlier, d, n, 0:sent, :]
-        passed[d, n, 0:sent, :] = total
-        send(bit, d, n).start()
-
-    rest = list(range(1, nblk))
-    for d in reversed(range(2, doms)):
-        gather(d, [0])
+    def beyond(d, n):
+        passed[d, n, 0:sent, :] = mine[d, n, 0:sent, :] + near_v[d, n, 0:sent, :]
+        pltpu.make_async_remote_copy(
+            src_ref=passed.at[d, n, pl.ds(0, sent)],
+            dst_ref=far_v.at[d // 2, n, pl.ds(0, sent)],
+            send_sem=tab_send.at[0],
+            recv_sem=far_recv.at[d // 2 - 1, n - 1],
+            device_id={"dom": me ^ d},
+            device_id_type=MESH,
+        ).start()
+
+    others = list(reversed(range(2, doms)))
+    gather([(d, 0) for d in others])
+    for d in others:
+        straight(d)
+    pairs = [(d, n) for n in range(1, nblk) for d in others]
+
+    @pl.when(jnp.logical_not(odd))
+    def _():
+        gather(pairs, beside)
 
     @pl.when(odd)
     def _():
-        for d in range(2, doms):
-            if d & 1:
-                send(0, d, 0).start()
-            else:
-                straight(d, 0)
-
-    @pl.when(jnp.logical_not(odd))
+        gather(pairs)
+
+    gather([(1, n) for n in range(nblk)])
+    for n in range(nblk):
+        beside(1, n)
+    gather([(0, n) for n in range(nblk)])
+
+    @pl.when(odd)
     def _():
-        for d in range(2, doms):
-            if d & 1:
-                straight(d, 0)
-
-    for d in reversed(range(2, doms)):
-        if d & 1:
-            gather(d, rest, lambda d, n: send(0, d, n).start())
-    for d in reversed(range(2, doms)):
-        if not d & 1:
-            gather(d, rest)
-    for bit in range(1, dom_bits):
-        for d in reversed(range(doms)):
-            if d % (1 << bit) == 0 and (d >> bit) & 1:
-                pl.when(jnp.logical_not(odd))(functools.partial(forward, bit, d, 0))
-                for n in rest:
-                    forward(bit, d, n)
+        for n in range(1, nblk):
+            settle(near_v.at[pl.ds(2, doms - 2), n, pl.ds(0, sent)], pass_recv.at[n - 1])
+            for d in others:
+                beyond(d, n)
+
     pl.semaphore_wait(gossip.at[0], around)
     greet(gossip.at[1])
-    gather(1, [0] + rest)
-    for n in [0] + rest:
-        send(0, 1, n).start()
-    gather(0, [0] + rest)
     settle(top_v.at[pl.ds(early, nblk - early), :, pl.ds(0, states), :], load_sem.at[4])
     convert(top_v, top_x, early, nblk)
     settle(bottom_v.at[:, :, pl.ds(0, states), :], load_sem.at[2])
@@ -288,18 +283,18 @@
 
     def block(n):
         tile = mine[0, n]
-        for bit in range(dom_bits):
-            tile = tile + got[bit, 0, n]
+        tile = tile + near_v[0, n]
         if n == 0:
             for d in range(2, doms):
                 tile = tile + lone[d]
-        turned = jnp.transpose(tile)
-        w_row = tile[states:states + 1, 0:pad]
-        l_high, l_low = split(turned[0:pad, :] * w_row)
+        else:
+            for k in range(1, doms // 2):
+                tile = tile + far_v[k, n]
+        l_high, l_low = split(tile[:, 0:pad])
         r_high, r_low = split(tile[:, pad:2 * pad])
         l_all = jnp.concatenate([l_high, l_high, l_low], axis=1)
         r_all = jnp.concatenate([r_high, r_high, r_low], axis=1)
-        expo = jnp.broadcast_to(turned[pad:2 * pad, states:states + 1], (pad, BLK))
+        expo = jnp.broadcast_to(tile[:, states:states + 1], (pad, BLK))
         power = expo * LOG2E
         for half in range(branches // 2):
             at = n * (branches // 2) + half
@@ -339,14 +334,10 @@
         )[0:1]
 
     def arrive(n):
-        for bit in range(1, dom_bits):
-            send(bit, 1 << bit, n).wait_recv()
-
-    @pl.when(odd)
-    def _():
-        settle(lone.at[pl.ds(2, doms - 2), pl.ds(0, sent)], near_recv.at[1])
-
-    pl.when(jnp.logical_not(odd))(functools.partial(arrive, 0))
+        for k in range(1, doms // 2):
+            settle(far_v.at[k, n, pl.ds(0, sent)], far_recv.at[k - 1, n - 1])
+
+    settle(lone.at[pl.ds(2, doms - 2), pl.ds(0, sent)], near_recv.at[1])
     alone = nblk // 2
     pl.semaphore_wait(gossip.at[1], around)
     greet(gossip.at[2])
@@ -354,7 +345,7 @@
         if n:
             arrive(n)
         else:
-            settle(got.at[0, 0, :, pl.ds(0, sent)], near_recv.at[0])
+            settle(near_v.at[0, :, pl.ds(0, sent)], near_recv.at[0])
         arrive(n + 1)
         block(n)
         block(n + 1)
@@ -387,7 +378,7 @@
     pay_v[rows - 1:rows, 0:late] = sums_of(rows - 1, min(2, group))[:, 0:late]
 
     peers = [(d, x, z) for d in range(doms) for x in range(inner) for z in range(outer)][1:]
-    peers.sort(key=lambda peer: -(min(peer[2], outer - peer[2]) + peer[1] + peer[0] // 2))
+    peers.sort(key=lambda peer: -(max(peer[2], -peer[2] % outer) + peer[1] + peer[0] // 2))
     for d, x, z in peers:
         pltpu.make_async_remote_copy(
             src_ref=pay_v.at[pl.ds(0, rows)],
@@ -450,11 +441,11 @@
         settle(req_v.at[pl.ds(1, doms - 1)], req_send.at[kind])
     settle(ids_v.at[pl.ds(1, sites - 1)], ids_send.at[0])
     settle(pay_in.at[pl.ds(0, (sites * doms - 1) * rows)], pay_send.at[0])
-    for i in range(2):
-        settle(lone.at[pl.ds(2, doms // 2 - 1), pl.ds(0, sent)], lone_send.at[i])
-    for d in range(1, doms):
-        start = 0 if d == 1 else 1
-        settle(mine.at[d, pl.ds(start, nblk - start), pl.ds(0, sent)], tab_send.at[d - 1])
+    settle(lone.at[pl.ds(2, doms - 2), pl.ds(0, sent)], lone_send.at[0])
+    settle(
+        mine.at[pl.ds(2, doms - 2), pl.ds(1, nblk - 1), pl.ds(0, sent)], tab_send.at[0]
+    )
+    settle(mine.at[1, :, pl.ds(0, sent)], tab_send.at[1])
 
 
 def store(loglik_v, share_v, new_v, loglik_ref, share_ref, new_ref, sem):
@@ -490,7 +481,6 @@
     owned = left_vectors.shape[0]
     tree = branch_lengths.shape[0]
     pad = round_up(states + 2, 64)
-    dom_bits = doms.bit_length() - 1
     inner = 2 if sites % 2 == 0 else 1
     outer = sites // inner
     held = round_up(owned, 8) + 8
@@ -520,7 +510,8 @@
             pltpu.SMEM((doms, 1, BLK), jnp.int32),
             pltpu.VMEM((doms, nblk) + tile, F32),
             pltpu.VMEM((doms, nblk) + tile, F32),
-            pltpu.VMEM((dom_bits, doms, nblk) + tile, F32),
+            pltpu.VMEM((doms, nblk) + tile, F32),
+            pltpu.VMEM((doms // 2, nblk) + tile, F32),
             pltpu.VMEM((doms,) + tile, F32),
             pltpu.VMEM((nblk * branches // 2, 2 * pad, 2 * BLK), BF16),
             pltpu.VMEM((nblk * branches // 2, 2 * pad, 2 * BLK), BF16),
@@ -545,11 +536,11 @@
             pltpu.SemaphoreType.REGULAR((outer,)),
             dma((2,)),
             dma((2,)),
-            dma((doms - 1,)),
             dma((2,)),
+            dma((1,)),
             dma((2,)),
-            dma((doms // 2 - 1, nblk)),
-            dma((dom_bits - 1, nblk)),
+            dma((nblk - 1,)),
+            dma((doms // 2 - 1, nblk - 1)),
             dma((1,)),
             dma((1,)),
             dma((1,)),

time: 23.4 us -> 22.7 us (0.970)
  Pallas kernels: 22.6 us -> 21.9 us
    pallas_call x1, Pallas kernels: 21.9 us -> 21.2 us  [on_device(): pl.pallas_call(functools.partial(body, cfg), out_shape=(pltpu.VMEM((branc...]
where the time goes in v3:
time: 22.7 us; the launch traced here: 22.5 us
  Pallas kernels  21.9 us (96%)
  between operations  0.64 us (3%)
    pallas_call x1, Pallas kernels, on_device(): pl.pallas_call(functools.partial(body, cfg), out_shape=(pltpu.VMEM((branc...  21.2 us
    pallas_call x1, Pallas kernels, on_device(): pl.pallas_call(store, out_shape=(jax.ShapeDtypeStruct((branches * nblk, B...  0.67 us

profile of v3, /device:TPU:0, one launch (start us, length us, event | category | flops | bytes accessed | tf_op | source)
XLA Modules:
  0.0 22.5 jit_solution(12829205440202200595)
XLA Ops:
  0.6 21.2 %shard_map.130 = (f32[128,128]{1,0:T(8,128)S(1)}, f32[32,64]{1,0:T(8,128)S(1)}, f32[1,1997]{1,0:T(1,128)S(1)}) custom-call(f32[16,61,8,128]{3,2,1,0:T(8,128)} %bitcast.9, f32[16,61,8,128]{3,2,1,0:T(8,128)} %bitcast.10, f32[61,64,61]{2,1,0:T(8,128)} %bitcast.11, f32[61,64,61]{2,1,0:T(8,128)} %bitcast.12, f32[64,61]{1,0:T(8,128)} %decay_hbm.1, ...), custom_call_target="tpu_custom_call" | custom-call | tf_op jit(solution)/shard_map/pallas_call | solution.py:496
  21.9 0.7 %shard_map.131 = (f32[128,128]{1,0:T(8,128)}, f32[32,64]{1,0:T(8,128)}, f32[1,1997]{1,0:T(1,128)}) custom-call(f32[128,128]{1,0:T(8,128)S(1)} %get-tuple-element.9.loglik_v, f32[32,64]{1,0:T(8,128)S(1)} %get-tuple-element.10.share_v, f32[1,1997]{1,0:T(1,128)S(1)} %get-tuple-element.11.new_v), custom_call_target="tpu_custom_call" | custom-call | tf_op jit(solution)/shard_map/pallas_call | solution.py:566

commit v4 on v3

--- a/solution.py
+++ b/solution.py
@@ -149,7 +149,7 @@
                 src_ref=req_v.at[0],
                 dst_ref=dest.at[delta],
                 send_sem=req_send.at[kind],
-                recv_sem=req_recv.at[kind],
+                recv_sem=req_recv.at[0 if kind else delta],
                 device_id={"dom": me ^ delta},
                 device_id_type=MESH,
             ).start()
@@ -175,7 +175,6 @@
     settle(tables_v.at[:, pl.ds(0, owned), :], load_sem.at[0])
     for load in small[1:]:
         load.wait()
-    settle(req_s.at[pl.ds(1, doms - 1)], req_recv.at[0])
 
     held = tables_v.shape[1]
     flat = tables_v.reshape(2 * states * held, states)
@@ -217,7 +216,7 @@
             src_ref=mine.at[d, n, pl.ds(0, sent)],
             dst_ref=near_v.at[d ^ 1, n, pl.ds(0, sent)],
             send_sem=tab_send.at[1 if d == 1 else 0],
-            recv_sem=near_recv.at[0] if d == 1 else pass_recv.at[n - 1],
+            recv_sem=near_recv.at[0] if d == 1 else pass_recv.at[(d ^ 1) - 2, n - 1],
             device_id={"dom": me ^ 1},
             device_id_type=MESH,
         ).start()
@@ -244,38 +243,38 @@
         ).start()
 
     others = list(reversed(range(2, doms)))
-    gather([(d, 0) for d in others])
-    for d in others:
-        straight(d)
-    pairs = [(d, n) for n in range(1, nblk) for d in others]
-
-    @pl.when(jnp.logical_not(odd))
-    def _():
-        gather(pairs, beside)
-
-    @pl.when(odd)
-    def _():
-        gather(pairs)
-
+    same = [d for d in others if not d & 1]
+    cross = [d for d in others if d & 1]
+
+    def serve(order, after):
+        for d in order:
+            settle(req_s.at[pl.ds(d, 1)], req_recv.at[d])
+            gather([(d, 0)])
+            straight(d)
+            gather([(d, n) for n in range(1, nblk)], after)
+
+    pl.when(odd)(functools.partial(serve, same + cross, None))
+    pl.when(jnp.logical_not(odd))(functools.partial(serve, cross + same, beside))
+    settle(req_s.at[pl.ds(1, 1)], req_recv.at[1])
     gather([(1, n) for n in range(nblk)])
     for n in range(nblk):
         beside(1, n)
-    gather([(0, n) for n in range(nblk)])
 
     @pl.when(odd)
     def _():
         for n in range(1, nblk):
-            settle(near_v.at[pl.ds(2, doms - 2), n, pl.ds(0, sent)], pass_recv.at[n - 1])
-            for d in others:
+            for d in (same + cross if n == 1 else cross + same):
+                settle(near_v.at[pl.ds(d, 1), n, pl.ds(0, sent)], pass_recv.at[d - 2, n - 1])
                 beyond(d, n)
 
+    gather([(0, n) for n in range(nblk)])
     pl.semaphore_wait(gossip.at[0], around)
     greet(gossip.at[1])
     settle(top_v.at[pl.ds(early, nblk - early), :, pl.ds(0, states), :], load_sem.at[4])
     convert(top_v, top_x, early, nblk)
     settle(bottom_v.at[:, :, pl.ds(0, states), :], load_sem.at[2])
     convert(bottom_v, bottom_x, 0, nblk)
-    settle(req_v.at[pl.ds(1, doms - 1)], req_recv.at[1])
+    settle(req_v.at[pl.ds(1, doms - 1)], req_recv.at[0])
     times = [lengths_s[chosen_s[b]] for b in range(branches)]
     for h in range(rows):
         parts_v[h, 0:2 * kinds, :] = jnp.zeros((2 * kinds, 2 * BLK), BF16)
@@ -535,11 +534,11 @@
             dma((7,)),
             pltpu.SemaphoreType.REGULAR((outer,)),
             dma((2,)),
-            dma((2,)),
+            dma((doms,)),
             dma((2,)),
             dma((1,)),
             dma((2,)),
-            dma((nblk - 1,)),
+            dma((doms - 2, nblk - 1)),
             dma((doms // 2 - 1, nblk - 1)),
             dma((1,)),
             dma((1,)),

time: 22.7 us -> 22.2 us (0.978)
  Pallas kernels: 21.9 us -> 21.5 us
    pallas_call x1, Pallas kernels: 21.2 us -> 20.8 us  [on_device(): pl.pallas_call(functools.partial(body, cfg), out_shape=(pltpu.VMEM((branc...]
where the time goes in v4:
time: 22.2 us; the launch traced here: 22.1 us
  Pallas kernels  21.5 us (97%)
  between operations  0.64 us (3%)
    pallas_call x1, Pallas kernels, on_device(): pl.pallas_call(functools.partial(body, cfg), out_shape=(pltpu.VMEM((branc...  20.8 us
    pallas_call x1, Pallas kernels, on_device(): pl.pallas_call(store, out_shape=(jax.ShapeDtypeStruct((branches * nblk, B...  0.67 us

profile of v4, /device:TPU:0, one launch (start us, length us, event | category | flops | bytes accessed | tf_op | source)
XLA Modules:
  0.0 22.1 jit_solution(10412066170862793241)
XLA Ops:
  0.6 20.8 %shard_map.130 = (f32[128,128]{1,0:T(8,128)S(1)}, f32[32,64]{1,0:T(8,128)S(1)}, f32[1,1997]{1,0:T(1,128)S(1)}) custom-call(f32[16,61,8,128]{3,2,1,0:T(8,128)} %bitcast.9, f32[16,61,8,128]{3,2,1,0:T(8,128)} %bitcast.10, f32[61,64,61]{2,1,0:T(8,128)} %bitcast.11, f32[61,64,61]{2,1,0:T(8,128)} %bitcast.12, f32[64,61]{1,0:T(8,128)} %decay_hbm.1, ...), custom_call_target="tpu_custom_call" | custom-call | tf_op jit(solution)/shard_map/pallas_call | solution.py:495
  21.4 0.7 %shard_map.131 = (f32[128,128]{1,0:T(8,128)}, f32[32,64]{1,0:T(8,128)}, f32[1,1997]{1,0:T(1,128)}) custom-call(f32[128,128]{1,0:T(8,128)S(1)} %get-tuple-element.9.loglik_v, f32[32,64]{1,0:T(8,128)S(1)} %get-tuple-element.10.share_v, f32[1,1997]{1,0:T(1,128)S(1)} %get-tuple-element.11.new_v), custom_call_target="tpu_custom_call" | custom-call | tf_op jit(solution)/shard_map/pallas_call | solution.py:565
